TPU v7x, 256 devices: a 2x2x32 block of a 4x8x32 slice. The times are simulated.
256 devices in a mesh: grp: 4 (over y, x), path: 32 (over z), amp: 2 (over core).
Axes of the slice: x: 2, y: 2, z: 32, core: 2. Of those that a mesh axis runs over, the one named last changes fastest.
The devices are a block of a 4x8x32 slice.
Arguments:
- left_slabs: bfloat16 [2048, 2, 16384], P(('grp', 'path'), None, 'amp'), parts along dimension 0, may hold values from -0.59765625 to 0.59765625
- right_slabs: bfloat16 [2048, 2, 8192], P(('grp', 'path'), None, 'amp'), parts along dimension 0, may hold values from -0.59765625 to 0.59765625
- term_index: int32 [2048], P(('grp', 'path')), parts along dimension 0, may hold values from 0 to 3
- left_terms: float32 [4, 2, 2, 2], replicated, may hold values from -4.2 to 4.2
- right_terms: float32 [4, 2, 2, 2], replicated, may hold values from -4.2 to 4.2
- left_gates: bfloat16 [2, 2, 128, 128], replicated, may hold values from -0.375 to 0.375
- right_gates: bfloat16 [2, 2, 128, 128], replicated, may hold values from -0.375 to 0.375
Outputs:
- amplitudes: bfloat16 [2, 65536, 8192], P(None, ('grp', 'path'), 'amp'), parts along dimension 1
There are 4 independent parts, one for each index of `grp`. A program takes and returns all parts, laid end to end along the dimension named above; an argument that names none is the same for every part. Nothing has to cross between parts.
All inputs are finite; a program needn't handle non-finite values.
Results may differ from a plain program's by a relative error of at most 0.0081.
Values may be sent and summed in bfloat16 or wider, within the bound.
A program may use at most 128 MiB of HBM per device.

v0:
```python
import jax
import jax.numpy as jnp
from jax import lax
from jax.sharding import PartitionSpec as P


def cut_along(value, dim, length):
    before, after = (value.shape[:dim], value.shape[dim + 1 :])
    return jnp.moveaxis(value.reshape(*before, length, -1, *after), dim, 0)


def edges_of(length, count):
    unit = 8 if length >= 8 * count else 1
    return [length // unit * k // count * unit for k in range(1, count)]


def in_order(blocks, dim):
    blocks = jnp.moveaxis(blocks, 0, dim)
    dims = blocks.shape
    return blocks.reshape(*dims[:dim], dims[dim] * dims[dim + 1], *dims[dim + 2 :])


def cut_exchange(value, axis, pieces, split_dim, concat_dim):
    blocks = cut_along(value, split_dim, lax.axis_size(axis))
    widest = max(range(1, max(2, blocks.ndim - 1)), key=lambda d: blocks.shape[d])
    finished = []
    for section in jnp.split(blocks, edges_of(blocks.shape[widest], pieces), axis=widest):
        if section.size:
            finished.append(lax.all_to_all(section, axis, split_axis=0, concat_axis=0, tiled=True))
    return in_order(jnp.concatenate(finished, axis=widest), concat_dim)


def from_everyone(value, axis):
    copies = jnp.broadcast_to(value, (lax.axis_size(axis), *value.shape))
    return lax.all_to_all(copies, axis, split_axis=0, concat_axis=0, tiled=True)


def gathered_copies(value, axis, dim):
    blocks = from_everyone(value, axis)
    return in_order(blocks, dim)


def cut_term(slab, term_mix):
    paths_here, _, length = slab.shape
    width = min(128, length)
    values = slab.astype(jnp.float32).reshape(paths_here, 2, length // width, width)
    identity = jnp.eye(width // 2, dtype=jnp.float32)

    def expand(part):
        return jnp.einsum("ab,nmj->najbm", identity, part).reshape(paths_here, width, width)

    real_kron = expand(term_mix[:, 0])
    imag_kron = expand(term_mix[:, 1])
    batch_dims = (((2,), (1,)), ((0,), (0,)))

    def times(rows, kron):
        return lax.dot_general(
            rows,
            kron,
            batch_dims,
            precision=lax.Precision.HIGHEST,
            preferred_element_type=jnp.float32,
        )

    real_rows = values[:, 0]
    imag_rows = values[:, 1]
    real_part = times(real_rows, real_kron) - times(imag_rows, imag_kron)
    imag_part = times(real_rows, imag_kron) + times(imag_rows, real_kron)
    return jnp.stack([real_part, imag_part], 1).reshape(paths_here, 2, length).astype(jnp.bfloat16)


def apply_low(slab, gate_mat):
    paths_here, _, length = slab.shape
    gate_width = gate_mat.shape[-1]
    real_rows = slab[:, 0].reshape(-1, gate_width)
    imag_rows = slab[:, 1].reshape(-1, gate_width)
    upper = jnp.concatenate([gate_mat[0].T, gate_mat[1].T], 1)
    lower = jnp.concatenate([-gate_mat[1].T, gate_mat[0].T], 1)
    right_matrix = jnp.concatenate([upper, lower], 0)
    product = jnp.dot(
        jnp.concatenate([real_rows, imag_rows], 1), right_matrix, preferred_element_type=jnp.float32
    )
    real_part = product[:, :gate_width].reshape(paths_here, length)
    imag_part = product[:, gate_width:].reshape(paths_here, length)
    return jnp.stack([real_part, imag_part], 1).astype(jnp.bfloat16)


def stack_matrix(gate_mat):
    upper = jnp.concatenate([gate_mat[0], -gate_mat[1]], 1)
    lower = jnp.concatenate([gate_mat[1], gate_mat[0]], 1)
    return jnp.concatenate([upper, lower], 0)


def gate_rows(matrix, data):
    batch = jnp.broadcast_to(matrix, (data.shape[0],) + matrix.shape)
    return lax.dot_general(
        batch, data, (((2,), (1,)), ((0,), (0,))), preferred_element_type=jnp.float32
    )


def right_high(moved, gate_mat):
    half_paths = moved.shape[0]
    gate_width = gate_mat.shape[-1]
    low_width = gate_width // 2
    data = moved.reshape(half_paths, gate_width, gate_width)
    blocks = gate_mat.reshape(2, low_width, 2, low_width, 2)
    rows_index = jnp.arange(gate_width, dtype=jnp.int32)[:, None]
    cols_index = jnp.arange(gate_width, dtype=jnp.int32)[None, :]
    same_slot = rows_index % low_width == cols_index % low_width
    total = jnp.zeros((half_paths, gate_width, gate_width), jnp.float32)
    for target in range(2):
        for source in range(2):
            select = (
                same_slot
                & (rows_index // low_width == source)
                & (cols_index // low_width == target)
            ).astype(jnp.bfloat16)
            placed = jnp.dot(
                data.reshape(-1, gate_width), select, preferred_element_type=jnp.float32
            )
            placed = placed.astype(jnp.bfloat16).reshape(half_paths, gate_width, gate_width)
            matrix = stack_matrix(blocks[:, :, target, :, source])
            total = total + gate_rows(matrix, placed)
    return total.astype(jnp.bfloat16).reshape(half_paths, 2, -1)


def contract(left_part, right_part):
    left_stack = jnp.concatenate([left_part[:, 0], left_part[:, 1]], 0)
    right_real = jnp.concatenate([right_part[:, 0], -right_part[:, 1]], 0)
    right_imag = jnp.concatenate([right_part[:, 1], right_part[:, 0]], 0)
    contract_dims = (((0,), (0,)), ((), ()))
    real_part = lax.dot_general(
        left_stack, right_real, contract_dims, preferred_element_type=jnp.float32
    )
    imag_part = lax.dot_general(
        left_stack, right_imag, contract_dims, preferred_element_type=jnp.float32
    )
    return (real_part, imag_part)


def mixes(term_index, terms):
    chosen = (term_index[:, None] == jnp.arange(terms.shape[0], dtype=jnp.int32)[None, :]).astype(
        jnp.float32
    )
    flat = jnp.dot(chosen, terms.reshape(terms.shape[0], 8), precision=lax.Precision.HIGHEST)
    return flat.reshape(-1, 2, 2, 2)


def shards(left_slabs, right_slabs, term_index, left_terms, right_terms, left_gates, right_gates):
    gate_width = left_gates.shape[-1]
    path_count = lax.axis_size("path")
    left = cut_term(left_slabs, mixes(term_index, left_terms))
    left = apply_low(left, left_gates[0])
    moved = lax.all_to_all(left, "amp", split_axis=0, concat_axis=2, tiled=True)
    half_paths = moved.shape[0]
    full_left = moved.shape[2]
    turned = gate_rows(
        stack_matrix(left_gates[1]),
        moved.reshape(half_paths, 2 * gate_width, full_left // gate_width),
    )
    turned = turned.astype(jnp.bfloat16).reshape(half_paths, 2, full_left)
    portion = cut_exchange(turned, "path", 2, 2, 0)
    rows_here = portion.shape[2]
    portion = portion.reshape(path_count, half_paths, 2, rows_here)
    row_block = gathered_copies(portion, "amp", 1).reshape(
        path_count * half_paths * 2, 2, rows_here
    )
    right = cut_term(right_slabs, mixes(term_index, right_terms))
    right = apply_low(right, right_gates[0])
    right_moved = lax.all_to_all(right, "amp", split_axis=0, concat_axis=2, tiled=True)
    right_turned = right_high(right_moved, right_gates[1])
    right = lax.all_to_all(right_turned, "amp", split_axis=2, concat_axis=0, tiled=True)
    everything = lax.all_gather(right, "path", axis=0, tiled=True)
    real_part, imag_part = contract(row_block, everything)
    return jnp.stack([real_part, imag_part], 0).astype(jnp.bfloat16)


def solution(mesh):
    return jax.shard_map(
        shards,
        mesh=mesh,
        in_specs=(
            P(("grp", "path"), None, "amp"),
            P(("grp", "path"), None, "amp"),
            P(("grp", "path")),
            P(),
            P(),
            P(),
            P(),
        ),
        out_specs=P(None, ("grp", "path"), "amp"),
        check_vma=False,
    )
```

profile of v0, /device:TPU:38, one launch (start us, length us, event | category | flops | bytes accessed | tf_op | source)
XLA Modules:
  0.0 335.3 jit_solution(4495637511785536944)
XLA Ops:
  6.6 0.8 slice_bitcast_fusion.16
  7.3 0.8 fusion.95
  8.1 0.8 fusion.82
  8.9 0.8 fusion.80
  9.8 18.9 %broadcast_multiply_fusion.3 = (f32[16,2,2,64,64]{0,1,4,2,3:T(2,128)}, f32[16,2,2,64,64]{0,1,4,2,3:T(2,128)}, f32[16,2,2,64,64]{0,1,4,2,3:T(2,128)}, f32[16,2,2,64,64]{0,1,4,2,3:T(2,128)}) fusion(f32[64,64]{1,0:T(8,128)S(1)} %fusion.75, f32[16,2,2]{0,1,2:T(2,128)S(1)} %copy.57, f32[16,2,2]{0,1,2:T(2,128)S(1)} %copy.60, f32[16,2,2]{0,1,2:T(2,128)S(1)} %copy.70, ...), kind=kLoop, calls=%fused_computation.18 | loop fusion | flops 1048576 | bytes 4211712 | tf_op jit(solution)/shard_map/ab,nmj->najbm/dot_general | solution.py:50
  28.7 5.3 %copy.72 = f32[16,128,128]{2,1,0:T(8,128)S(1)} copy(f32[16,128,128]{0,2,1:T(8,128)} %bitcast.164) | data formatting | bytes 2097152 | tf_op jit(solution)/shard_map/reshape | solution.py:50
  33.9 0.2 reshape.225
  34.1 5.2 %copy.74 = f32[16,128,128]{2,1,0:T(8,128)S(1)} copy(f32[16,128,128]{0,2,1:T(8,128)} %bitcast.163) | data formatting | bytes 2097152 | tf_op jit(solution)/shard_map/reshape | solution.py:50
  39.4 0.6 fusion.54
  40.0 0.6 fusion.53
  40.6 0.6 fusion.23
  41.2 0.6 fusion.24
  41.8 0.3 convolution_convert_fusion.6
  42.3 1.3 pad_maximum_fusion.6
  43.6 3.5 %all-to-all-start.4 = ((bf16[16,2,4096]{2,1,0:T(2,128)(2,1)}), bf16[16,2,4096]{2,1,0:T(2,128)(2,1)S(1)}, u32[]{:S(2)}, u32[]{:S(2)}) async-start(bf16[16,2,4096]{2,1,0:T(2,128)(2,1)} %pad_maximum_fusion.6), calls=%async_computation.4 | async-start | bytes 524288 | tf_op jit(solution)/shard_map/all_to_all | solution.py:170
  47.1 0.2 all-gather.2.cloned.1.call-start
  47.3 1.3 all-to-all-done.4
  48.6 0.1 copy.98
  48.7 0.3 copy.80
  49.0 0.2 reshape_reshape.14
  49.2 0.3 convolution_convert_fusion.5
  49.5 0.3 convolution_convert_fusion.4
  49.8 0.3 convolution_convert_fusion.3
  50.1 0.3 convolution_convert_fusion.2
  50.5 10.0 %reshape_squeeze.17 = bf16[2,64,2,64,2]{4,3,2,1,0:T(8,128)(2,1)} reshape(bf16[1,2,128,128]{3,2,1,0:T(8,128)(2,1)S(1)} %slice-done) | data formatting | bytes 131072 | tf_op jit(solution)/shard_map/reshape;squeeze | solution.py:106
  60.5 8.1 %slice_reduce_fusion = (bf16[64,64]{1,0:T(8,128)(2,1)S(1)}, bf16[64,64]{1,0:T(8,128)(2,1)S(1)}, bf16[64,64]{1,0:T(8,128)(2,1)S(1)}, bf16[64,64]{1,0:T(8,128)(2,1...) fusion(bf16[2,64,2,64,2]{4,3,2,1,0:T(8,128)(2,1)} %reshape_sque, ...), kind=kLoop, calls=%fused_computation.38 | loop fusion | bytes 131072 | tf_op jit(solution)/shard_map/slice | solution.py:89
  68.7 0.2 fusion.51
  69.0 0.2 convolution_add_fusion.3
  69.3 0.2 convolution_add_fusion.2
  69.5 0.2 fusion.22
  69.8 6.8 %copy.81 = bf16[8,2,8192]{0,1,2:T(2,128)(2,1)} copy(bf16[8,2,8192]{2,1,0:T(2,128)(2,1)S(1)} %reshape.222) | data formatting | bytes 524288 | tf_op jit(solution)/shard_map/reshape | solution.py:124
  76.6 6.1 %reshape.234 = bf16[2,2,32768]{2,1,0:T(2,128)(2,1)S(1)} reshape(bf16[8192,2,8]{2,1,0:T(2,128)(2,1)} %bitcast.165) | data formatting | bytes 524288
  82.8 4.0 %all_to_all.63 = bf16[2,2,32768]{2,1,0:T(2,128)(2,1)S(1)} all-to-all(bf16[2,2,32768]{2,1,0:T(2,128)(2,1)S(1)} %reshape.234), channel_id=1, replica_groups=mesh['grp'=4,'path'=32,'amp'=2] {'amp'}, dimensions={0} | all-to-all | bytes 524288 | tf_op jit(solution)/shard_map/all_to_all | solution.py:172
  86.7 6.1 %reshape.235 = bf16[8192,2,8]{2,1,0:T(2,128)(2,1)} reshape(bf16[2,2,32768]{2,1,0:T(2,128)(2,1)S(1)} %all_to_all.63) | data formatting | bytes 524288
  92.9 9.3 %copy.83 = bf16[2,8,2,4096]{3,1,0,2:T(8,128)(2,1)} copy(bf16[2,8,2,4096]{1,2,3,0:T(2,128)(2,1)} %bitcast.166) | data formatting | bytes 524288 | tf_op jit(solution)/shard_map/all_to_all | solution.py:172
  102.3 5.3 %copy.59 = f32[16,128,128]{2,1,0:T(8,128)S(1)} copy(f32[16,128,128]{0,2,1:T(8,128)} %bitcast.162) | data formatting | bytes 2097152 | tf_op jit(solution)/shard_map/reshape | solution.py:50
  107.5 0.4 reshape.224
  107.9 5.2 %copy.61 = f32[16,128,128]{2,1,0:T(8,128)S(1)} copy(f32[16,128,128]{0,2,1:T(8,128)} %bitcast.161) | data formatting | bytes 2097152 | tf_op jit(solution)/shard_map/reshape | solution.py:50
  113.2 0.6 fusion.33
  113.8 0.6 fusion.32
  114.5 0.6 fusion.20
  115.1 0.6 fusion.21
  115.7 0.3 convolution_convert_fusion
  116.1 0.1 stack_reshape.20
  116.3 0.1 stack_reshape.21
  116.4 1.2 pad_maximum_fusion.4
  117.6 4.2 %all_to_all.64 = bf16[16,2,8192]{2,1,0:T(2,128)(2,1)S(1)} all-to-all(bf16[16,2,8192]{2,1,0:T(2,128)(2,1)S(1)} %pad_maximum_fusion.4), channel_id=1, replica_groups=mesh['grp'=4,'path'=32,'amp'=2] {'amp'}, dimensions={0} | all-to-all | bytes 1048576 | tf_op jit(solution)/shard_map/all_to_all | solution.py:154
  121.8 0.5 copy.97
  122.3 0.4 reshape.213
  122.8 0.4 convolution_convert_fusion.1
  123.2 0.3 reshape_reshape.12
  123.5 0.5 copy.96
  124.1 0.4 fusion.97
  124.4 77.7 %all_to_all.65 = bf16[32,4,2,512]{3,2,1,0:T(2,128)(2,1)S(1)} all-to-all(bf16[32,4,2,512]{3,2,1,0:T(2,128)(2,1)S(1)} %get-tuple-element.17), channel_id=1, replica_groups=mesh['grp'=4,'path'=32,'amp'=2] {'path'}, dimensions={0} | all-to-all | bytes 524288 | tf_op jit(solution)/shard_map/all_to_all | solution.py:29
  202.1 48.5 %all_to_all.66 = bf16[32,4,2,512]{3,2,1,0:T(2,128)(2,1)S(1)} all-to-all(bf16[32,4,2,512]{3,2,1,0:T(2,128)(2,1)S(1)} %get-tuple-element.18), channel_id=1, replica_groups=mesh['grp'=4,'path'=32,'amp'=2] {'path'}, dimensions={0} | all-to-all | bytes 524288 | tf_op jit(solution)/shard_map/all_to_all | solution.py:29
  250.6 0.7 pad_maximum_fusion.5
  251.5 4.6 %all_to_all.67 = bf16[2,32,8,2,512]{4,2,1,3,0:T(8,128)(2,1)S(1)} all-to-all(bf16[2,32,8,2,512]{4,2,1,3,0:T(8,128)(2,1)S(1)} %broadcast_in_dim.25), channel_id=1, replica_groups=mesh['grp'=4,'path'=32,'amp'=2] {'amp'}, dimensions={0} | all-to-all | bytes 2097152 | tf_op jit(solution)/shard_map/all_to_all | solution.py:35
  256.3 48.4 %all-gather.2.cloned.1.call-done = bf16[512,2,4096]{2,0,1:T(8,128)(2,1)} async-done(((bf16[16,2,4096]{2,0,1:T(8,128)(2,1)}), bf16[512,2,4096]{2,0,1:T(8,128)(2,1)}) %all-gather.2.cloned.1.call-update) | async-done | bytes 8388624 | tf_op jit(solution)/shard_map/all_gather | solution.py:173
  304.7 3.9 %slice_bitcast_fusion = (bf16[512,4096]{1,0:T(8,128)(2,1)S(1)}, bf16[512,4096]{1,0:T(8,128)(2,1)S(1)}) fusion(bf16[512,2,4096]{2,0,1:T(8,128)(2,1)} %all-gather.2.cloned.1.call-done), kind=kLoop, calls=%fused_computation.13 | loop fusion | bytes 16777216 | tf_op jit(solution)/shard_map/squeeze | solution.py:129
  308.6 1.9 copy-done.2
  310.5 0.3 fusion.96
  310.8 4.9 %fusion.14 = bf16[1,512,4096]{2,1,0:T(8,128)(2,1)S(1)} fusion(bf16[512,4096]{1,0:T(8,128)(2,1)S(1)} %fusion.96, bf16[512,4096]{1,0:T(8,128)(2,1)S(1)} %get-tuple-element.14, bf16[512,512]{1,0:T(8,128)(2,1)S(1)} %get-tuple-element.16, bf16[512,512]{1,0:T(8,128)(2,1)S(1)} %get-tuple-element.15), kind=kOutput, calls=%fused_computation.11 | convolution fusion | flops 4315938816 | bytes 13631488 | tf_op jit(solution)/shard_map/dot_general | solution.py:132
  315.8 6.3 %fusion.17 = bf16[1,512,4096]{2,1,0:T(8,128)(2,1)} fusion(bf16[512,4096]{1,0:T(8,128)(2,1)S(1)} %get-tuple-element.14, bf16[512,4096]{1,0:T(8,128)(2,1)S(1)} %get-tuple-element.13, bf16[512,512]{1,0:T(8,128)(2,1)S(1)} %get-tuple-element.16, bf16[512,512]{1,0:T(8,128)(2,1)S(1)} %get-tuple-element.15), kind=kOutput, calls=%fused_computation.12 | convolution fusion | flops 4315938816 | bytes 13631488 | tf_op jit(solution)/shard_map/dot_general | solution.py:135
  322.1 6.3 %pad_maximum_fusion = bf16[2,512,4096]{2,1,0:T(8,128)(2,1)} fusion(bf16[1,512,4096]{2,1,0:T(8,128)(2,1)} %fusion.17, bf16[1,512,4096]{2,1,0:T(8,128)(2,1)S(1)} %fusion.14), kind=kLoop, calls=%fused_computation.8 | loop fusion | flops 4194304 | bytes 16777216 | tf_op jit(solution)/shard_map/stack | solution.py:175
  (42 shorter events, 1.0 us)
Async XLA Ops:
  6.5 1.6 copy-start
  28.7 5.3 %copy-start.5 = (bf16[16,2,4096]{2,1,0:T(2,128)(2,1)S(1)}, bf16[16,2,4096]{2,1,0:T(2,128)(2,1)}, u32[]{:S(2)}) copy-start(bf16[16,2,4096]{2,1,0:T(2,128)(2,1)} %param.8) | copy-start | bytes 786436
  39.4 11.1 %slice-start = ((bf16[2,2,128,128]{3,2,1,0:T(8,128)(2,1)}), bf16[1,2,128,128]{3,2,1,0:T(8,128)(2,1)S(1)}, s32[]{:S(2)}) async-start(bf16[2,2,128,128]{3,2,1,0:T(8,128)(2,1)} %param.13), calls=%async_computation.7 | async-start | bytes 131072 | tf_op jit(solution)/shard_map/slice | solution.py:171
  43.6 5.0 %all-to-all-start.4 = ((bf16[16,2,4096]{2,1,0:T(2,128)(2,1)}), bf16[16,2,4096]{2,1,0:T(2,128)(2,1)S(1)}, u32[]{:S(2)}, u32[]{:S(2)}) async-start(bf16[16,2,4096]{2,1,0:T(2,128)(2,1)} %pad_maximum_fusion.6), calls=%async_computation.4 | async-start | bytes 524288 | tf_op jit(solution)/shard_map/all_to_all | solution.py:170
  47.1 257.6 %all-gather.2.cloned.1.call-start = ((), (), s32[]{:S(2)}) async-start(), calls=%async_computation.6 | async-start | bytes 8650752 | tf_op jit(solution)/shard_map/all_gather | solution.py:173
  86.7 20.8 %copy-start.3 = (bf16[16,2,8192]{2,1,0:T(2,128)(2,1)S(1)}, bf16[16,2,8192]{2,1,0:T(2,128)(2,1)}, u32[]{:S(2)}) copy-start(bf16[16,2,8192]{2,1,0:T(2,128)(2,1)} %param.7) | copy-start | bytes 1572868
  102.2 10.9 %copy-start.4 = (bf16[2,2,128,128]{3,2,1,0:T(8,128)(2,1)S(1)}, bf16[2,2,128,128]{3,2,1,0:T(8,128)(2,1)}, u32[]{:S(2)}) copy-start(bf16[2,2,128,128]{3,2,1,0:T(8,128)(2,1)} %param.12) | copy-start | bytes 393220
  304.7 5.8 %copy-start.2 = (bf16[512,2,4096]{2,0,1:T(8,128)(2,1)S(1)}, bf16[512,2,4096]{2,0,1:T(8,128)(2,1)}, u32[]{:S(2)}) copy-start(bf16[512,2,4096]{2,0,1:T(8,128)(2,1)} %all-gather.2.cloned.1.call-done) | copy-start | bytes 25165828
  315.8 12.7 %copy-start.1 = (f32[4,2,2,2]{0,3,2,1:T(2,128)S(1)}, f32[4,2,2,2]{0,3,2,1:T(2,128)}, u32[]{:S(2)}) copy-start(f32[4,2,2,2]{0,3,2,1:T(2,128)} %param.10) | copy-start | bytes 388
Sparse Core Ops, SparseCore 0:
  102.4 202.2 all-gather.1
where the time goes:
time: 336 us; the launch traced here: 335 us
  blocking collectives  139 us (41%)
  local copies, waits for them, and re-layouts  78.4 us (23%)
  waiting for transfers between devices  49.7 us (15%)
  other arithmetic  29.7 us (9%)
  matrix products  20.9 us (6%)
  between operations  13.9 us (4%)
  starting transfers between devices  3.71 us (1%)
    all_to_all x2, blocking collectives, cut_exchange(): lax.all_to_all(section, axis, split_axis=0, concat_axis=0, tiled=True)  126 us
    all_gather x1, waiting for transfers between devices, shards(): everything = lax.all_gather(right, 'path', axis=0, tiled=True)  48.4 us
    reshape x4, local copies, waits for them, and re-layouts, expand(): jnp.einsum('ab,nmj->najbm', identity, part)  21 us
    dot_general x1, other arithmetic, expand(): jnp.einsum('ab,nmj->najbm', identity, part)  18.9 us
    unnamed x14, local copies, waits for them, and re-layouts  14.2 us
    another operation x1, local copies, waits for them, and re-layouts, right_high(): blocks = gate_mat.reshape(2, low_width, 2, low_width, 2)  10 us
    all_to_all x1, local copies, waits for them, and re-layouts, shards(): lax.all_to_all(right_turned, 'amp', split_axis=2, concat_axis=0, tiled=True)  9.31 us
    slice x1, local copies, waits for them, and re-layouts, stack_matrix(): upper = jnp.concatenate([gate_mat[0], -gate_mat[1]], 1)  8.08 us
  transfers between devices with their start and end apart: 2, of which 2 were waited for; matrix products, arithmetic and copies ran while one was open for 6% of the time, Pallas kernels for 0%

commit v1 on v0

v1 whole, which is shorter than its diff:
```python
import functools

import jax
import jax.numpy as jnp
from jax import lax
from jax.experimental import pallas as pl
from jax.experimental.pallas import tpu as pltpu
from jax.sharding import PartitionSpec as P

MESH = pl.DeviceIdType.MESH
F32 = jnp.float32
BF16 = jnp.bfloat16
PIECES = 4
NT = (((1,), (1,)), ((), ()))
TN = (((0,), (0,)), ((), ()))


def dot(a, b, dims=(((1,), (0,)), ((), ()))):
    return lax.dot_general(a, b, dims, preferred_element_type=F32)


def grid2(rows, cols):
    return (
        lax.broadcasted_iota(jnp.int32, (rows, cols), 0),
        lax.broadcasted_iota(jnp.int32, (rows, cols), 1),
    )


def one_hot(cond):
    return jnp.where(cond, 1.0, 0.0).astype(BF16)


def stack_matrix(re, im):
    upper = jnp.concatenate([re, -im], 1)
    lower = jnp.concatenate([im, re], 1)
    return jnp.concatenate([upper, lower], 0)


def coefficients(idx_ref, term_ref, path, even):
    base = idx_ref[path] * 8
    pick = lambda c, m, j: term_ref[base + (c * 4 + m * 2 + j)]
    spread = lambda s0, s1: jnp.where(even, s0, s1)
    return (
        spread(pick(0, 0, 0), pick(0, 1, 1)),
        spread(pick(1, 0, 0), pick(1, 1, 1)),
        spread(pick(0, 0, 1), pick(0, 1, 0)),
        spread(pick(1, 0, 1), pick(1, 1, 0)),
    )


def cut_paths(slab, first_path, idx_ref, term_ref, pair_swap, even):
    paths, _, rows, width = slab.shape
    flat = slab.reshape(paths * 2 * rows, width)
    swapped = dot(flat, pair_swap)
    wide = flat.astype(F32)
    done = []
    for p in range(paths):
        at = 2 * p * rows
        xr, xi = wide[at : at + rows], wide[at + rows : at + 2 * rows]
        sr, si = swapped[at : at + rows], swapped[at + rows : at + 2 * rows]
        ar, ai, br, bi = coefficients(idx_ref, term_ref, first_path + p, even)
        cr = (xr * ar + sr * br) - (xi * ai + si * bi)
        ci = (xr * ai + sr * bi) + (xi * ar + si * br)
        done.append(jnp.concatenate([cr, ci], 1).astype(BF16))
    return jnp.concatenate(done, 0)


def exchange_kernel(
    chips,
    idx_ref, lterm_ref, rterm_ref,
    left_ref, right_ref, lgate_ref, rgate_ref,
    lall_ref, rall_ref,
    lx, rx, lt, rt, lsend, rown, up, down,
    swap_send, swap_recv,
    ag_send, ag_recv, aa_send, aa_recv, pr_send, pr_recv, loc_sem, rloc_sem,
):
    me = lax.axis_index("path")
    core = lax.axis_index("amp")
    nxt, prv = lax.rem(me + 1, chips), lax.rem(me + chips - 1, chips)
    peer = {"amp": 1 - core}
    toward = ({"path": nxt}, {"path": prv})
    half = chips // 2
    pieces = rown.shape[0]

    barrier = pltpu.get_barrier_semaphore()
    for who in (peer, *toward):
        pl.semaphore_signal(barrier, inc=1, device_id=who, device_id_type=MESH)
    pl.semaphore_wait(barrier, 3)

    mine = lx.shape[0]
    lrows, rrows = left_ref.shape[2], right_ref.shape[2]
    rplace = pl.ds(pl.multiple_of(core * rrows, rrows), rrows)
    lplace = pl.ds(pl.multiple_of(core * lrows, lrows), lrows)
    give_right = pltpu.make_async_remote_copy(
        src_ref=right_ref, dst_ref=rx.at[:, :, rplace],
        send_sem=swap_send.at[0], recv_sem=swap_recv.at[0], device_id=peer, device_id_type=MESH)
    give_left = pltpu.make_async_remote_copy(
        src_ref=left_ref.at[pl.ds((1 - core) * mine, mine)], dst_ref=lx.at[:, :, lplace],
        send_sem=swap_send.at[1], recv_sem=swap_recv.at[1], device_id=peer, device_id_type=MESH)
    give_right.start()
    give_left.start()
    rx[:, :, rplace] = right_ref[...]
    lx[:, :, lplace] = left_ref[pl.ds(core * mine, mine)]

    row, col = grid2(128, 128)
    pair_swap = one_hot(row == (col ^ 1))
    even = (lax.broadcasted_iota(jnp.int32, (1, 128), 1) & 1) == 0
    prow, pcol = grid2(256, 256)
    regroup = one_hot(pcol == (prow % 8) * 32 + prow // 8)

    s_low = stack_matrix(rgate_ref[0, 0], rgate_ref[0, 1])
    s_low = jnp.concatenate(
        [s_low, s_low[64:128], s_low[0:64], s_low[192:256], s_low[128:192]], 0)
    here = rrows
    full = 2 * here
    srow, scol = grid2(here, 128)
    krow, kcol = grid2(2 * full, 128)
    parts = []
    for c in range(2):
        gate = rgate_ref[1, c]
        rows_of = []
        for t in range(2):
            pick_rows = one_hot(scol == 2 * (core * here + srow) + t)
            pick_cols = one_hot(kcol == 2 * (krow % full) + (krow // full + t) % 2)
            some = dot(pick_rows, gate).astype(BF16)
            rows_of.append(dot(some, pick_cols, NT).astype(BF16))
        parts.append(jnp.concatenate(rows_of, 0))
    s_high = stack_matrix(parts[0], parts[1])

    give_right.wait_recv()
    low_lanes = lax.broadcasted_iota(jnp.int32, (1, 128), 1) < 64
    step = 4
    for first in range(0, rx.shape[0], step):
        cut = cut_paths(rx[first : first + step], first, idx_ref, rterm_ref, pair_swap, even)
        low = dot(cut, s_low, NT).astype(BF16)
        tall = []
        for p in range(step):
            at = low[p * full : (p + 1) * full]
            tall.append(jnp.concatenate(
                [at[:, 0:128], at[:, 256:384], at[:, 128:256], at[:, 384:512]], 0))
        turned = dot(s_high, jnp.concatenate(tall, 1))
        for p in range(step):
            z = turned[:, p * 128 : (p + 1) * 128]
            q = first + p
            for c in range(2):
                at = 2 * c * here
                pair = jnp.where(low_lanes, z[at : at + here], z[at + here : at + 2 * here])
                rt[c, q // 8, (q % 8) * 32 : (q % 8) * 32 + here] = pair.astype(BF16)
    per_piece = here // pieces
    for g in range(2):
        both = [dot(regroup, rt[c, g]) for c in range(2)]
        for r in range(here):
            tile = jnp.concatenate([b[r * 8 : r * 8 + 8] for b in both], 0).astype(BF16)
            at = (r % per_piece) * 128
            rown[r // per_piece, g * 16 : g * 16 + 16, at : at + 128] = tile

    def chunk(d, s):
        return lax.rem(me + (chips - s if d == 0 else s), chips)

    def gather_copy(d, s, j):
        at = chunk(d, s)
        src = rown.at[j] if s == 0 else rall_ref.at[at, j]
        return pltpu.make_async_remote_copy(
            src_ref=src, dst_ref=rall_ref.at[at, j],
            send_sem=ag_send.at[d, s, j], recv_sem=ag_recv.at[d, s, j],
            device_id=toward[d], device_id_type=MESH)

    def gather_arrival(d, s, j):
        at = chunk(d, s + 1)
        return pltpu.make_async_remote_copy(
            src_ref=rall_ref.at[at, j], dst_ref=rall_ref.at[at, j],
            send_sem=ag_send.at[d, s, j], recv_sem=ag_recv.at[d, s, j],
            device_id=toward[d], device_id_type=MESH)

    gather_steps = (half - 1, half)

    def gather_step(s):
        @pl.loop(0, pieces)
        def _(j):
            for d in range(2):
                if 1 <= s <= gather_steps[d]:
                    gather_arrival(d, s - 1, j).wait_recv()
                if s < gather_steps[d]:
                    gather_copy(d, s, j).start()

    gather_step(0)
    keep_own = pltpu.make_async_copy(rown, rall_ref.at[me], rloc_sem)
    keep_own.start()

    s_low = stack_matrix(lgate_ref[0, 0], lgate_ref[0, 1])
    s_high = stack_matrix(lgate_ref[1, 0], lgate_ref[1, 1])
    give_left.wait_recv()
    step = 2
    groups = 4
    for first in range(0, mine, step):
        cut = cut_paths(
            lx[first : first + step], core * mine + first, idx_ref, lterm_ref, pair_swap, even)
        low = dot(cut, s_low, NT).astype(BF16)
        tall = [
            jnp.concatenate([low[p * 128 : (p + 1) * 128, c * 128 : (c + 1) * 128] for c in range(2)], 0)
            for p in range(step)
        ]
        turned = dot(s_high, jnp.concatenate(tall, 1)).astype(BF16)
        for p in range(step):
            for c in range(2):
                for g in range(groups):
                    at = c * 128 + g * 32
                    lt[c, g, (first + p) * 32 : (first + p) * 32 + 32] = (
                        turned[at : at + 32, p * 128 : (p + 1) * 128])
    per_chip = 128 // chips
    for g in range(groups):
        both = [dot(regroup, lt[c, g]) for c in range(2)]
        for r in range(32):
            m = g * 32 + r
            tile = jnp.concatenate([b[r * 8 : r * 8 + 8] for b in both], 0).astype(BF16)
            slot = lax.rem(m // per_chip - me + chips, chips)
            at = (m % per_chip) * 128
            lsend[slot, :, at : at + 128] = tile

    counts = ([half - s for s in range(half)], [half - 1 - s for s in range(half - 1)])
    bases = [[sum(c[:s]) for s in range(len(c))] for c in counts]
    landing = (up, down)

    def block_copy(d, s):
        n = counts[d][s]
        if s == 0:
            src = lsend.at[pl.ds(1, n)] if d == 0 else lsend.at[pl.ds(half + 1, n)]
        else:
            src = landing[d].at[pl.ds(bases[d][s - 1] + (1 if d == 0 else 0), n)]
        return pltpu.make_async_remote_copy(
            src_ref=src, dst_ref=landing[d].at[pl.ds(bases[d][s], n)],
            send_sem=aa_send.at[d, s], recv_sem=aa_recv.at[d, s],
            device_id=toward[d], device_id_type=MESH)

    def keep(src, at, n):
        here_copy = pltpu.make_async_copy(src, lall_ref.at[at, core], loc_sem.at[n])
        there_copy = pltpu.make_async_remote_copy(
            src_ref=src, dst_ref=lall_ref.at[at, core],
            send_sem=pr_send.at[n], recv_sem=pr_recv.at[n], device_id=peer, device_id_type=MESH)
        here_copy.start()
        there_copy.start()
        return here_copy, there_copy

    kept = []
    for s in range(half + 1):
        if s >= 1:
            gather_step(s)
        for d in range(2):
            if 1 <= s <= len(counts[d]):
                block_copy(d, s - 1).wait_recv()
            if s < len(counts[d]):
                block_copy(d, s).start()
            if s == 0 and d == 0:
                kept.append(keep(lsend.at[0], me, 0))
            if 1 <= s <= len(counts[d]):
                at = bases[d][s - 1] + (0 if d == 0 else counts[d][s - 1] - 1)
                kept.append(keep(landing[d].at[at], chunk(d, s), len(kept)))

    give_right.wait_send()
    give_left.wait_send()
    keep_own.wait()
    for s in range(half):
        @pl.loop(0, pieces)
        def _(j):
            for d in range(2):
                if s < gather_steps[d]:
                    gather_copy(d, s, j).wait_send()
        for d in range(2):
            if s < len(counts[d]):
                block_copy(d, s).wait_send()
    for here_copy, there_copy in kept:
        here_copy.wait()
        there_copy.wait()


def product_kernel(left_ref, right_ref, out_ref, lhs):
    rows = left_ref.shape[1]
    depth = left_ref.shape[0]

    @pl.when((pl.program_id(0) == 0) & (pl.program_id(1) == 0))
    def _():
        row, col = grid2(256, 256)
        imag = (row // 8) % 2 == 1
        signed = jnp.where(row == col, jnp.where(imag, -1.0, 1.0), 0.0).astype(BF16)
        crossed = one_hot(row == (col ^ 8))
        for k in range(0, depth, 256):
            part = left_ref[k : k + 256]
            lhs[0:rows, k : k + 256] = dot(part, signed, TN).astype(BF16)
            lhs[rows : 2 * rows, k : k + 256] = dot(part, crossed, TN).astype(BF16)

    right = right_ref[...].reshape(depth, right_ref.shape[-1])
    out_ref[0] = dot(lhs[0:rows], right).astype(BF16)
    out_ref[1] = dot(lhs[rows : 2 * rows], right).astype(BF16)


def shards(left_slabs, right_slabs, term_index, left_terms, right_terms, left_gates, right_gates):
    chips = lax.axis_size("path")
    paths = left_slabs.shape[0]
    mine = paths // 2
    left = left_slabs.reshape(paths, 2, -1, 128)
    right = right_slabs.reshape(paths, 2, -1, 128)
    lrows, rrows = left.shape[2], right.shape[2]
    half = chips // 2
    pieces = PIECES
    cols = rrows * 128
    block = 2 * lrows * 128 // chips
    vmem = pl.BlockSpec(memory_space=pltpu.VMEM)
    smem = pl.BlockSpec(memory_space=pltpu.SMEM)
    hbm = pl.BlockSpec(memory_space=pl.ANY)
    dma = pltpu.SemaphoreType.DMA
    left_all, right_all = pl.pallas_call(
        functools.partial(exchange_kernel, chips),
        out_shape=(
            jax.ShapeDtypeStruct((chips, 2, 2 * mine, block), BF16),
            jax.ShapeDtypeStruct((chips, pieces, 2 * paths, cols // pieces), BF16),
        ),
        in_specs=[smem, smem, smem, vmem, vmem, vmem, vmem],
        out_specs=(hbm, hbm),
        scratch_shapes=[
            pltpu.VMEM((mine, 2, 2 * lrows, 128), BF16),
            pltpu.VMEM((paths, 2, 2 * rrows, 128), BF16),
            pltpu.VMEM((2, 4, 256, 128), BF16),
            pltpu.VMEM((2, 2, 256, 128), BF16),
            pltpu.VMEM((chips, 2 * mine, block), BF16),
            pltpu.VMEM((pieces, 2 * paths, cols // pieces), BF16),
            pltpu.VMEM((half * (half + 1) // 2, 2 * mine, block), BF16),
            pltpu.VMEM((half * (half - 1) // 2, 2 * mine, block), BF16),
            dma((2,)), dma((2,)),
            dma((2, half, pieces)), dma((2, half, pieces)),
            dma((2, half)), dma((2, half)),
            dma((chips,)), dma((chips,)), dma((chips,)), dma,
        ],
        compiler_params=pltpu.CompilerParams(
            collective_id=0, has_side_effects=True, vmem_limit_bytes=40 * 1024 * 1024),
        name="exchange",
    )(
        term_index, left_terms.reshape(-1), right_terms.reshape(-1),
        left, right, left_gates, right_gates,
    )
    depth = chips * 2 * paths
    tile = min(512, cols // pieces)
    per = cols // pieces // tile
    return pl.pallas_call(
        product_kernel,
        grid=(pieces, per),
        out_shape=jax.ShapeDtypeStruct((2, block, cols), BF16),
        in_specs=[
            pl.BlockSpec((depth, block), lambda j, k: (0, 0)),
            pl.BlockSpec((chips, 1, 2 * paths, tile), lambda j, k: (0, j, 0, k)),
        ],
        out_specs=pl.BlockSpec((2, block, tile), lambda j, k: (0, 0, j * per + k)),
        scratch_shapes=[pltpu.VMEM((2 * block, depth), BF16)],
        compiler_params=pltpu.CompilerParams(vmem_limit_bytes=40 * 1024 * 1024),
        name="product",
    )(left_all.reshape(depth, block), right_all)


def solution(mesh):
    return jax.shard_map(
        shards,
        mesh=mesh,
        in_specs=(
            P(("grp", "path"), None, "amp"),
            P(("grp", "path"), None, "amp"),
            P(("grp", "path")),
            P(),
            P(),
            P(),
            P(),
        ),
        out_specs=P(None, ("grp", "path"), "amp"),
        check_vma=False,
    )
```

time: 336 us -> 189 us (0.56)
  Pallas kernels: 0 us -> 180 us
  blocking collectives: 139 us -> 0 us
  local copies, waits for them, and re-layouts: 78.4 us -> 6.82 us
  waiting for transfers between devices: 49.7 us -> 0 us
  other arithmetic: 29.7 us -> 0 us
  matrix products: 20.9 us -> 0 us
  between operations: 13.9 us -> 0.03 us
  starting transfers between devices: 3.71 us -> 0 us
    pallas_call x0 -> x2, Pallas kernels: none -> 180 us  [the longest x1 168 us: shards(): pl.pallas_call(functools.partial(exchange_kernel, chips), out_shape=(jax....]
    all_to_all x5 -> x0, blocking collectives: 139 us -> none  [the longest x2 126 us: cut_exchange(): lax.all_to_all(section, axis, split_axis=0, concat_axis=0, tiled=True)]
    all_gather x1 -> x0, waiting for transfers between devices: 48.4 us -> none  [shards(): everything = lax.all_gather(right, 'path', axis=0, tiled=True)]
    reshape x9 -> x4, local copies, waits for them, and re-layouts: 28.9 us -> 2.78 us  [the longest x1 1.44 us: shards(): left = left_slabs.reshape(paths, 2, -1, 128)]
    dot_general x23 -> x0, matrix products: 20.9 us -> none  [the longest x1 6.3 us: contract(): lax.dot_general(left_stack, right_imag, contract_dims, preferred_element_...]
    dot_general x1 -> x0, other arithmetic: 18.9 us -> none  [expand(): jnp.einsum('ab,nmj->najbm', identity, part)]
    another operation x8 -> x0, local copies, waits for them, and re-layouts: 11.5 us -> none  [the longest x1 10 us: right_high(): blocks = gate_mat.reshape(2, low_width, 2, low_width, 2)]
    all_to_all x5 -> x0, local copies, waits for them, and re-layouts: 10.4 us -> none  [the longest x1 9.31 us: shards(): lax.all_to_all(right_turned, 'amp', split_axis=2, concat_axis=0, tiled=True)]
  transfers between devices with their start and end apart: 2 -> 0, of which waited for: 2 -> 0; matrix products, arithmetic and copies ran while one was open for 6% -> 0% of each run, Pallas kernels for 0% -> 0%
where the time goes in v1:
time: 189 us; the launch traced here: 187 us
  Pallas kernels  180 us (95%)
  local copies, waits for them, and re-layouts  6.82 us (4%)
    pallas_call x1, Pallas kernels, shards(): pl.pallas_call(functools.partial(exchange_kernel, chips), out_shape=(jax....  168 us
    pallas_call x1, Pallas kernels, shards(): pl.pallas_call(product_kernel, grid=(pieces, per), out_shape=jax.ShapeDty...  12.5 us
    unnamed x8, local copies, waits for them, and re-layouts  4.04 us

profile of v1, /device:TPU:38, one launch (start us, length us, event | category | flops | bytes accessed | tf_op | source)
XLA Modules:
  0.0 187.2 jit_solution(13917982436206124144)
XLA Ops:
  0.0 0.8 copy.10
  0.8 0.1 reshape.15.lterm_ref
  0.9 0.8 copy.11
  1.7 0.1 reshape.16.rterm_ref
  1.8 1.2 reshape.18.right_ref
  2.9 1.4 reshape.17.left_ref
  4.4 0.0 copy-start
  4.4 0.9 copy-done
  5.3 0.0 copy-start.1
  5.3 0.9 copy-done.1
  6.2 0.0 copy-start.2
  6.2 0.7 copy-done.2
  6.8 167.8 %exchange.1 = (bf16[32,2,16,512]{3,2,1,0:T(8,128)(2,1)S(1)}, bf16[32,4,32,1024]{3,2,1,0:T(8,128)(2,1)S(1)}) custom-call(s32[16]{0:T(128)S(1)} %copy-done.2, f32[32]{0:T(128)S(1)} %reshape.15.lterm_ref, f32[32]{0:T(128)S(1)} %reshape.16.rterm_ref, bf16[16,2,64,128]{3,2,1,0:T(8,128)(2,1)S(1)} %reshape.17.left_ref, ...), custom_call_target="tpu_custom_call" | custom-call | tf_op jit(solution)/shard_map/exchange/pallas_call | solution.py:311
  174.7 12.5 %product.1 = bf16[2,512,4096]{2,1,0:T(8,128)(2,1)} custom-call(bf16[1024,512]{1,0:T(8,128)(2,1)S(1)} %bitcast.1, bf16[32,4,32,1024]{3,2,1,0:T(8,128)(2,1)S(1)} %get-tuple-element.8.right_ref), custom_call_target="tpu_custom_call" | custom-call | tf_op jit(solution)/shard_map/product/pallas_call | solution.py:343
Async XLA Ops:
  4.4 0.9 copy-start
  5.3 0.9 copy-start.1
  6.2 0.7 copy-start.2

commit v2 on v1

--- a/solution.py
+++ b/solution.py
@@ -10,7 +10,7 @@
 MESH = pl.DeviceIdType.MESH
 F32 = jnp.float32
 BF16 = jnp.bfloat16
-PIECES = 4
+VMEM_LIMIT = 24 * 1024 * 1024
 NT = (((1,), (1,)), ((), ()))
 TN = (((0,), (0,)), ((), ()))
 
@@ -37,8 +37,8 @@
 
 
 def coefficients(idx_ref, term_ref, path, even):
-    base = idx_ref[path] * 8
-    pick = lambda c, m, j: term_ref[base + (c * 4 + m * 2 + j)]
+    term = idx_ref[path]
+    pick = lambda c, m, j: term_ref[c, m, j, term]
     spread = lambda s0, s1: jnp.where(even, s0, s1)
     return (
         spread(pick(0, 0, 0), pick(0, 1, 1)),
@@ -67,12 +67,13 @@
 
 def exchange_kernel(
     chips,
-    idx_ref, lterm_ref, rterm_ref,
-    left_ref, right_ref, lgate_ref, rgate_ref,
-    lall_ref, rall_ref,
-    lx, rx, lt, rt, lsend, rown, up, down,
-    swap_send, swap_recv,
-    ag_send, ag_recv, aa_send, aa_recv, pr_send, pr_recv, loc_sem, rloc_sem,
+    idx_hbm, lterm_hbm, rterm_hbm,
+    left_ref, right_ref, lgate_hbm, rgate_hbm,
+    total_ref, last_ref, lhs_ref,
+    idx_ref, lterm_ref, rterm_ref, lgate_ref, rgate_ref,
+    lx, rx, lt, rt, lsend, early, up, down, peer_blocks, own_blocks, lhs_now,
+    in_sem, swap_send, swap_recv,
+    ag_send, ag_recv, aa_send, aa_recv, pr_send, pr_recv,
 ):
     me = lax.axis_index("path")
     core = lax.axis_index("amp")
@@ -80,11 +81,20 @@
     peer = {"amp": 1 - core}
     toward = ({"path": nxt}, {"path": prv})
     half = chips // 2
-    pieces = rown.shape[0]
+    pieces, wide = early.shape[1], early.shape[3]
+    held = early.shape[0]
 
     barrier = pltpu.get_barrier_semaphore()
     for who in (peer, *toward):
         pl.semaphore_signal(barrier, inc=1, device_id=who, device_id_type=MESH)
+    loads = [
+        pltpu.make_async_copy(src, dst, in_sem.at[n])
+        for n, (src, dst) in enumerate((
+            (rgate_hbm, rgate_ref), (idx_hbm, idx_ref), (rterm_hbm, rterm_ref),
+            (lterm_hbm, lterm_ref), (lgate_hbm, lgate_ref)))
+    ]
+    for load in loads:
+        load.start()
     pl.semaphore_wait(barrier, 3)
 
     mine = lx.shape[0]
@@ -102,6 +112,8 @@
     rx[:, :, rplace] = right_ref[...]
     lx[:, :, lplace] = left_ref[pl.ds(core * mine, mine)]
 
+    for load in loads[:3]:
+        load.wait()
     row, col = grid2(128, 128)
     pair_swap = one_hot(row == (col ^ 1))
     even = (lax.broadcasted_iota(jnp.int32, (1, 128), 1) & 1) == 0
@@ -152,40 +164,45 @@
         for r in range(here):
             tile = jnp.concatenate([b[r * 8 : r * 8 + 8] for b in both], 0).astype(BF16)
             at = (r % per_piece) * 128
-            rown[r // per_piece, g * 16 : g * 16 + 16, at : at + 128] = tile
-
-    def chunk(d, s):
-        return lax.rem(me + (chips - s if d == 0 else s), chips)
+            early[0, r // per_piece, g * 16 : g * 16 + 16, at : at + 128] = tile
+
+    def slot_of(d, s):
+        return min(2 * s - (1 - d), chips - 1) if s else 0
+
+    def right_slot(n):
+        return early.at[n] if n < held else last_ref.at[n - held]
 
     def gather_copy(d, s, j):
-        at = chunk(d, s)
-        src = rown.at[j] if s == 0 else rall_ref.at[at, j]
         return pltpu.make_async_remote_copy(
-            src_ref=src, dst_ref=rall_ref.at[at, j],
+            src_ref=right_slot(slot_of(d, s)).at[j], dst_ref=right_slot(slot_of(d, s + 1)).at[j],
             send_sem=ag_send.at[d, s, j], recv_sem=ag_recv.at[d, s, j],
             device_id=toward[d], device_id_type=MESH)
 
-    def gather_arrival(d, s, j):
-        at = chunk(d, s + 1)
-        return pltpu.make_async_remote_copy(
-            src_ref=rall_ref.at[at, j], dst_ref=rall_ref.at[at, j],
-            send_sem=ag_send.at[d, s, j], recv_sem=ag_recv.at[d, s, j],
-            device_id=toward[d], device_id_type=MESH)
-
     gather_steps = (half - 1, half)
-
-    def gather_step(s):
+    group = chips // 4
+    slice_cols = wide // pieces
+
+    def add_slice(g, piece, j):
+        at = pl.ds(pl.multiple_of(j * slice_cols, slice_cols), slice_cols)
+        right = early[g * group : (g + 1) * group, piece, :, at].reshape(-1, slice_cols)
+        to = pl.ds(pl.multiple_of(piece * wide + j * slice_cols, slice_cols), slice_cols)
+        more = dot(lhs_now[...], right)
+        total_ref[:, to] = more if g == 0 else total_ref[:, to] + more
+
+    def gather_step(s, work=None):
         @pl.loop(0, pieces)
         def _(j):
             for d in range(2):
                 if 1 <= s <= gather_steps[d]:
-                    gather_arrival(d, s - 1, j).wait_recv()
+                    gather_copy(d, s - 1, j).wait_recv()
                 if s < gather_steps[d]:
                     gather_copy(d, s, j).start()
+            if work is not None:
+                add_slice(*work, j)
 
     gather_step(0)
-    keep_own = pltpu.make_async_copy(rown, rall_ref.at[me], rloc_sem)
-    keep_own.start()
+    for load in loads[3:]:
+        load.wait()
 
     s_low = stack_matrix(lgate_ref[0, 0], lgate_ref[0, 1])
     s_high = stack_matrix(lgate_ref[1, 0], lgate_ref[1, 1])
@@ -232,33 +249,60 @@
             send_sem=aa_send.at[d, s], recv_sem=aa_recv.at[d, s],
             device_id=toward[d], device_id_type=MESH)
 
-    def keep(src, at, n):
-        here_copy = pltpu.make_async_copy(src, lall_ref.at[at, core], loc_sem.at[n])
-        there_copy = pltpu.make_async_remote_copy(
-            src_ref=src, dst_ref=lall_ref.at[at, core],
+    handed = []
+
+    def hand_over(src, n):
+        there = pltpu.make_async_remote_copy(
+            src_ref=src, dst_ref=peer_blocks.at[n],
             send_sem=pr_send.at[n], recv_sem=pr_recv.at[n], device_id=peer, device_id_type=MESH)
-        here_copy.start()
-        there_copy.start()
-        return here_copy, there_copy
-
-    kept = []
-    for s in range(half + 1):
-        if s >= 1:
-            gather_step(s)
+        there.start()
+        handed.append((n, there))
+        own_blocks[n] = src[...]
+
+    def block_step(s):
         for d in range(2):
             if 1 <= s <= len(counts[d]):
                 block_copy(d, s - 1).wait_recv()
             if s < len(counts[d]):
                 block_copy(d, s).start()
             if s == 0 and d == 0:
-                kept.append(keep(lsend.at[0], me, 0))
+                hand_over(lsend.at[0], 0)
             if 1 <= s <= len(counts[d]):
                 at = bases[d][s - 1] + (0 if d == 0 else counts[d][s - 1] - 1)
-                kept.append(keep(landing[d].at[at], chunk(d, s), len(kept)))
+                hand_over(landing[d].at[at], slot_of(d, s) if s < half else chips - 1)
+
+    krow, kcol = grid2(16 * 2 * group, 16 * 2 * group)
+    imag = (krow // 8) % 2 == 1
+    signed = jnp.where(krow == kcol, jnp.where(imag, -1.0, 1.0), 0.0).astype(BF16)
+    crossed = one_hot(krow == (kcol ^ 8))
+
+    def build_lhs(g, to_ref):
+        rows = []
+        for n in range(g * group, (g + 1) * group):
+            dict(handed)[n].wait_recv()
+            own, other = own_blocks[n], peer_blocks[n]
+            first = core == 0
+            rows.append(jnp.where(first, own, other))
+            rows.append(jnp.where(first, other, own))
+        block = jnp.concatenate(rows, 0)
+        to_ref[0 : block.shape[1]] = dot(block, signed, TN).astype(BF16)
+        to_ref[block.shape[1] :] = dot(block, crossed, TN).astype(BF16)
+
+    block_step(0)
+    quarter = half // 4
+    for s in range(1, half + 1):
+        ready, phase = divmod(s - 1, quarter)
+        if s == half:
+            block_step(s)
+            build_lhs(3, lhs_ref)
+        if phase == 0 and ready >= 1:
+            build_lhs(ready - 1, lhs_now)
+        gather_step(s, (ready - 1, phase) if ready >= 1 else None)
+        if s < half:
+            block_step(s)
 
     give_right.wait_send()
     give_left.wait_send()
-    keep_own.wait()
     for s in range(half):
         @pl.loop(0, pieces)
         def _(j):
@@ -268,29 +312,31 @@
         for d in range(2):
             if s < len(counts[d]):
                 block_copy(d, s).wait_send()
-    for here_copy, there_copy in kept:
-        here_copy.wait()
-        there_copy.wait()
-
-
-def product_kernel(left_ref, right_ref, out_ref, lhs):
-    rows = left_ref.shape[1]
-    depth = left_ref.shape[0]
-
-    @pl.when((pl.program_id(0) == 0) & (pl.program_id(1) == 0))
-    def _():
-        row, col = grid2(256, 256)
-        imag = (row // 8) % 2 == 1
-        signed = jnp.where(row == col, jnp.where(imag, -1.0, 1.0), 0.0).astype(BF16)
-        crossed = one_hot(row == (col ^ 8))
-        for k in range(0, depth, 256):
-            part = left_ref[k : k + 256]
-            lhs[0:rows, k : k + 256] = dot(part, signed, TN).astype(BF16)
-            lhs[rows : 2 * rows, k : k + 256] = dot(part, crossed, TN).astype(BF16)
-
-    right = right_ref[...].reshape(depth, right_ref.shape[-1])
-    out_ref[0] = dot(lhs[0:rows], right).astype(BF16)
-    out_ref[1] = dot(lhs[rows : 2 * rows], right).astype(BF16)
+    for _, there in handed:
+        there.wait_send()
+
+
+def finish_kernel(total_ref, last_ref, lhs_ref, out_ref, staged, sems):
+    count, _, rows, tile = staged.shape
+    per = last_ref.shape[3] // tile
+
+    def put(k):
+        to = pl.ds(pl.multiple_of(k * tile, tile), tile)
+        return pltpu.make_async_copy(staged.at[k], out_ref.at[:, :, to], sems.at[k])
+
+    @pl.loop(0, count)
+    def _(k):
+        at = pl.ds(pl.multiple_of(lax.rem(k, per) * tile, tile), tile)
+        right = last_ref[:, k // per, :, at].reshape(-1, tile)
+        to = pl.ds(pl.multiple_of(k * tile, tile), tile)
+        for c in range(2):
+            part = slice(c * rows, (c + 1) * rows)
+            staged[k, c] = (total_ref[part, to] + dot(lhs_ref[part], right)).astype(BF16)
+        put(k).start()
+
+    @pl.loop(0, count)
+    def _(k):
+        put(k).wait()
 
 
 def shards(left_slabs, right_slabs, term_index, left_terms, right_terms, left_gates, right_gates):
@@ -301,58 +347,69 @@
     right = right_slabs.reshape(paths, 2, -1, 128)
     lrows, rrows = left.shape[2], right.shape[2]
     half = chips // 2
-    pieces = PIECES
+    pieces = half // 4
     cols = rrows * 128
     block = 2 * lrows * 128 // chips
     vmem = pl.BlockSpec(memory_space=pltpu.VMEM)
-    smem = pl.BlockSpec(memory_space=pltpu.SMEM)
-    hbm = pl.BlockSpec(memory_space=pl.ANY)
+    hbm = pl.BlockSpec(memory_space=pltpu.HBM)
     dma = pltpu.SemaphoreType.DMA
-    left_all, right_all = pl.pallas_call(
+    held = chips // 4 * 3
+    wide = cols // pieces
+    depth = chips // 4 * 2 * paths
+    blocks = (2 * mine, block)
+    total, last, lhs = pl.pallas_call(
         functools.partial(exchange_kernel, chips),
         out_shape=(
-            jax.ShapeDtypeStruct((chips, 2, 2 * mine, block), BF16),
-            jax.ShapeDtypeStruct((chips, pieces, 2 * paths, cols // pieces), BF16),
+            jax.ShapeDtypeStruct((2 * block, cols), F32),
+            jax.ShapeDtypeStruct((chips - held, pieces, 2 * paths, wide), BF16),
+            jax.ShapeDtypeStruct((2 * block, depth), BF16),
         ),
-        in_specs=[smem, smem, smem, vmem, vmem, vmem, vmem],
-        out_specs=(hbm, hbm),
+        in_specs=[hbm, hbm, hbm, vmem, vmem, hbm, hbm],
+        out_specs=(vmem, vmem, vmem),
         scratch_shapes=[
+            pltpu.SMEM((paths,), jnp.int32),
+            pltpu.SMEM((2, 2, 2, 4), F32),
+            pltpu.SMEM((2, 2, 2, 4), F32),
+            pltpu.VMEM(left_gates.shape, BF16),
+            pltpu.VMEM(right_gates.shape, BF16),
             pltpu.VMEM((mine, 2, 2 * lrows, 128), BF16),
             pltpu.VMEM((paths, 2, 2 * rrows, 128), BF16),
             pltpu.VMEM((2, 4, 256, 128), BF16),
             pltpu.VMEM((2, 2, 256, 128), BF16),
-            pltpu.VMEM((chips, 2 * mine, block), BF16),
-            pltpu.VMEM((pieces, 2 * paths, cols // pieces), BF16),
-            pltpu.VMEM((half * (half + 1) // 2, 2 * mine, block), BF16),
-            pltpu.VMEM((half * (half - 1) // 2, 2 * mine, block), BF16),
-            dma((2,)), dma((2,)),
+            pltpu.VMEM((chips, *blocks), BF16),
+            pltpu.VMEM((held, pieces, 2 * paths, wide), BF16),
+            pltpu.VMEM((half * (half + 1) // 2, *blocks), BF16),
+            pltpu.VMEM((half * (half - 1) // 2, *blocks), BF16),
+            pltpu.VMEM((chips, *blocks), BF16),
+            pltpu.VMEM((chips, *blocks), BF16),
+            pltpu.VMEM((2 * block, depth), BF16),
+            dma((5,)), dma((2,)), dma((2,)),
             dma((2, half, pieces)), dma((2, half, pieces)),
             dma((2, half)), dma((2, half)),
-            dma((chips,)), dma((chips,)), dma((chips,)), dma,
+            dma((chips,)), dma((chips,)),
         ],
         compiler_params=pltpu.CompilerParams(
-            collective_id=0, has_side_effects=True, vmem_limit_bytes=40 * 1024 * 1024),
+            collective_id=0, has_side_effects=True, vmem_limit_bytes=VMEM_LIMIT),
         name="exchange",
     )(
-        term_index, left_terms.reshape(-1), right_terms.reshape(-1),
-        left, right, left_gates, right_gates,
+        *(pltpu.with_memory_space_constraint(x, pltpu.HBM) for x in (
+            term_index, jnp.transpose(left_terms, (1, 2, 3, 0)), jnp.transpose(right_terms, (1, 2, 3, 0)))),
+        left, right,
+        *(pltpu.with_memory_space_constraint(x, pltpu.HBM) for x in (left_gates, right_gates)),
     )
-    depth = chips * 2 * paths
-    tile = min(512, cols // pieces)
-    per = cols // pieces // tile
+    tile = min(512, wide)
     return pl.pallas_call(
-        product_kernel,
-        grid=(pieces, per),
+        finish_kernel,
         out_shape=jax.ShapeDtypeStruct((2, block, cols), BF16),
-        in_specs=[
-            pl.BlockSpec((depth, block), lambda j, k: (0, 0)),
-            pl.BlockSpec((chips, 1, 2 * paths, tile), lambda j, k: (0, j, 0, k)),
+        in_specs=[vmem, vmem, vmem],
+        out_specs=hbm,
+        scratch_shapes=[
+            pltpu.VMEM((cols // tile, 2, block, tile), BF16),
+            pltpu.SemaphoreType.DMA((cols // tile,)),
         ],
-        out_specs=pl.BlockSpec((2, block, tile), lambda j, k: (0, 0, j * per + k)),
-        scratch_shapes=[pltpu.VMEM((2 * block, depth), BF16)],
-        compiler_params=pltpu.CompilerParams(vmem_limit_bytes=40 * 1024 * 1024),
-        name="product",
-    )(left_all.reshape(depth, block), right_all)
+        compiler_params=pltpu.CompilerParams(vmem_limit_bytes=16 * 1024 * 1024),
+        name="finish",
+    )(total, last, lhs)
 
 
 def solution(mesh):

time: 189 us -> 178 us (0.942)
  Pallas kernels: 180 us -> 173 us
  local copies, waits for them, and re-layouts: 6.82 us -> 2.59 us
    pallas_call x1, Pallas kernels: 12.5 us -> 4.6 us  [shards(): pl.pallas_call(finish_kernel, out_shape=jax.ShapeDtypeStruct((2, block, c...]
    unnamed x8 -> x0, local copies, waits for them, and re-layouts: 4.04 us -> none
where the time goes in v2:
time: 178 us; the launch traced here: 175 us
  Pallas kernels  173 us (97%)
  local copies, waits for them, and re-layouts  2.59 us (1%)
    pallas_call x1, Pallas kernels, shards(): pl.pallas_call(functools.partial(exchange_kernel, chips), out_shape=(jax....  168 us
    pallas_call x1, Pallas kernels, shards(): pl.pallas_call(finish_kernel, out_shape=jax.ShapeDtypeStruct((2, block, c...  4.6 us

profile of v2, /device:TPU:38, one launch (start us, length us, event | category | flops | bytes accessed | tf_op | source)
XLA Modules:
  0.0 175.4 jit_solution(12616146803689482354)
XLA Ops:
  0.0 1.2 reshape.7.right_ref
  1.2 1.4 reshape.6.left_ref
  2.6 168.2 %exchange.1 = (f32[1024,4096]{1,0:T(8,128)S(1)}, bf16[8,4,32,1024]{3,2,1,0:T(8,128)(2,1)S(1)}, bf16[1024,256]{1,0:T(8,128)(2,1)S(1)}) custom-call(s32[16]{0:T(128)} %idx_hbm.1, f32[2,2,2,4]{3,2,1,0:T(2,128)} %bitcast.2, f32[2,2,2,4]{3,2,1,0:T(2,128)} %bitcast.3, bf16[16,2,64,128]{3,2,1,0:T(8,128)(2,1)S(1)} %reshape.6.left_ref, ...), custom_call_target="tpu_custom_call" | custom-call | tf_op jit(solution)/shard_map/exchange/pallas_call | solution.py:360
  170.8 4.6 %finish.1 = bf16[2,512,4096]{2,1,0:T(8,128)(2,1)} custom-call(f32[1024,4096]{1,0:T(8,128)S(1)} %get-tuple-element.8.total_ref, bf16[8,4,32,1024]{3,2,1,0:T(8,128)(2,1)S(1)} %get-tuple-element.9.last_ref, bf16[1024,256]{1,0:T(8,128)(2,1)S(1)} %get-tuple-element.10.lhs_ref), custom_call_target="tpu_custom_call" | custom-call | tf_op jit(solution)/shard_map/finish/pallas_call | solution.py:401

commit v3 on v2

--- a/solution.py
+++ b/solution.py
@@ -68,10 +68,10 @@
 def exchange_kernel(
     chips,
     idx_hbm, lterm_hbm, rterm_hbm,
-    left_ref, right_ref, lgate_hbm, rgate_hbm,
+    left_hbm, right_hbm, lgate_hbm, rgate_hbm,
     total_ref, last_ref, lhs_ref,
     idx_ref, lterm_ref, rterm_ref, lgate_ref, rgate_ref,
-    lx, rx, lt, rt, lsend, early, up, down, peer_blocks, own_blocks, lhs_now,
+    lraw, rraw, lx, rx, lt, rt, lsend, early, up, down, peer_blocks, own_blocks, lhs_now,
     in_sem, swap_send, swap_recv,
     ag_send, ag_recv, aa_send, aa_recv, pr_send, pr_recv,
 ):
@@ -87,32 +87,38 @@
     barrier = pltpu.get_barrier_semaphore()
     for who in (peer, *toward):
         pl.semaphore_signal(barrier, inc=1, device_id=who, device_id_type=MESH)
+    mine = lx.shape[0]
     loads = [
         pltpu.make_async_copy(src, dst, in_sem.at[n])
         for n, (src, dst) in enumerate((
+            (right_hbm, rraw.at[:, core]),
             (rgate_hbm, rgate_ref), (idx_hbm, idx_ref), (rterm_hbm, rterm_ref),
-            (lterm_hbm, lterm_ref), (lgate_hbm, lgate_ref)))
+            (lterm_hbm, lterm_ref), (lgate_hbm, lgate_ref),
+            (left_hbm.at[pl.ds(core * mine, mine)], lraw.at[:, core])))
     ]
     for load in loads:
         load.start()
     pl.semaphore_wait(barrier, 3)
 
-    mine = lx.shape[0]
-    lrows, rrows = left_ref.shape[2], right_ref.shape[2]
-    rplace = pl.ds(pl.multiple_of(core * rrows, rrows), rrows)
-    lplace = pl.ds(pl.multiple_of(core * lrows, lrows), lrows)
+    rrows, lrows = rx.shape[2] // 2, lx.shape[2] // 2
     give_right = pltpu.make_async_remote_copy(
-        src_ref=right_ref, dst_ref=rx.at[:, :, rplace],
+        src_ref=right_hbm, dst_ref=rraw.at[:, core],
         send_sem=swap_send.at[0], recv_sem=swap_recv.at[0], device_id=peer, device_id_type=MESH)
     give_left = pltpu.make_async_remote_copy(
-        src_ref=left_ref.at[pl.ds((1 - core) * mine, mine)], dst_ref=lx.at[:, :, lplace],
+        src_ref=left_hbm.at[pl.ds((1 - core) * mine, mine)], dst_ref=lraw.at[:, core],
         send_sem=swap_send.at[1], recv_sem=swap_recv.at[1], device_id=peer, device_id_type=MESH)
     give_right.start()
     give_left.start()
-    rx[:, :, rplace] = right_ref[...]
-    lx[:, :, lplace] = left_ref[pl.ds(core * mine, mine)]
-
-    for load in loads[:3]:
+
+    def to_rows(raw, full, part, count):
+        @pl.loop(0, raw.shape[0], unroll=4)
+        def _(p):
+            at = pl.ds(pl.multiple_of(part * count, count), count)
+            full[p, :, at] = raw[p, part].reshape(2, count, 128)
+
+    loads[0].wait()
+    to_rows(rraw, rx, core, rrows)
+    for load in loads[1:4]:
         load.wait()
     row, col = grid2(128, 128)
     pair_swap = one_hot(row == (col ^ 1))
@@ -140,6 +146,7 @@
     s_high = stack_matrix(parts[0], parts[1])
 
     give_right.wait_recv()
+    to_rows(rraw, rx, 1 - core, rrows)
     low_lanes = lax.broadcasted_iota(jnp.int32, (1, 128), 1) < 64
     step = 4
     for first in range(0, rx.shape[0], step):
@@ -201,12 +208,14 @@
                 add_slice(*work, j)
 
     gather_step(0)
-    for load in loads[3:]:
+    for load in loads[4:]:
         load.wait()
 
     s_low = stack_matrix(lgate_ref[0, 0], lgate_ref[0, 1])
     s_high = stack_matrix(lgate_ref[1, 0], lgate_ref[1, 1])
     give_left.wait_recv()
+    for part in range(2):
+        to_rows(lraw, lx, part, lrows)
     step = 2
     groups = 4
     for first in range(0, mine, step):
@@ -343,9 +352,7 @@
     chips = lax.axis_size("path")
     paths = left_slabs.shape[0]
     mine = paths // 2
-    left = left_slabs.reshape(paths, 2, -1, 128)
-    right = right_slabs.reshape(paths, 2, -1, 128)
-    lrows, rrows = left.shape[2], right.shape[2]
+    lrows, rrows = left_slabs.shape[2] // 128, right_slabs.shape[2] // 128
     half = chips // 2
     pieces = half // 4
     cols = rrows * 128
@@ -364,7 +371,7 @@
             jax.ShapeDtypeStruct((chips - held, pieces, 2 * paths, wide), BF16),
             jax.ShapeDtypeStruct((2 * block, depth), BF16),
         ),
-        in_specs=[hbm, hbm, hbm, vmem, vmem, hbm, hbm],
+        in_specs=[hbm] * 7,
         out_specs=(vmem, vmem, vmem),
         scratch_shapes=[
             pltpu.SMEM((paths,), jnp.int32),
@@ -372,6 +379,8 @@
             pltpu.SMEM((2, 2, 2, 4), F32),
             pltpu.VMEM(left_gates.shape, BF16),
             pltpu.VMEM(right_gates.shape, BF16),
+            pltpu.VMEM((mine, 2, 2, lrows * 128), BF16),
+            pltpu.VMEM((paths, 2, 2, rrows * 128), BF16),
             pltpu.VMEM((mine, 2, 2 * lrows, 128), BF16),
             pltpu.VMEM((paths, 2, 2 * rrows, 128), BF16),
             pltpu.VMEM((2, 4, 256, 128), BF16),
@@ -383,7 +392,7 @@
             pltpu.VMEM((chips, *blocks), BF16),
             pltpu.VMEM((chips, *blocks), BF16),
             pltpu.VMEM((2 * block, depth), BF16),
-            dma((5,)), dma((2,)), dma((2,)),
+            dma((7,)), dma((2,)), dma((2,)),
             dma((2, half, pieces)), dma((2, half, pieces)),
             dma((2, half)), dma((2, half)),
             dma((chips,)), dma((chips,)),
@@ -393,9 +402,8 @@
         name="exchange",
     )(
         *(pltpu.with_memory_space_constraint(x, pltpu.HBM) for x in (
-            term_index, jnp.transpose(left_terms, (1, 2, 3, 0)), jnp.transpose(right_terms, (1, 2, 3, 0)))),
-        left, right,
-        *(pltpu.with_memory_space_constraint(x, pltpu.HBM) for x in (left_gates, right_gates)),
+            term_index, jnp.transpose(left_terms, (1, 2, 3, 0)), jnp.transpose(right_terms, (1, 2, 3, 0)),
+            left_slabs, right_slabs, left_gates, right_gates)),
     )
     tile = min(512, wide)
     return pl.pallas_call(

time: 178 us -> 175 us (0.983)
  local copies, waits for them, and re-layouts: 2.59 us -> 0 us
    reshape x2 -> x0, local copies, waits for them, and re-layouts: 2.59 us -> none  [the longest x1 1.44 us: shards(): left = left_slabs.reshape(paths, 2, -1, 128)]
where the time goes in v3:
time: 175 us; the launch traced here: 173 us
  Pallas kernels  173 us (99%)
    pallas_call x1, Pallas kernels, shards(): pl.pallas_call(functools.partial(exchange_kernel, chips), out_shape=(jax....  168 us
    pallas_call x1, Pallas kernels, shards(): pl.pallas_call(finish_kernel, out_shape=jax.ShapeDtypeStruct((2, block, c...  4.6 us

profile of v3, /device:TPU:38, one launch (start us, length us, event | category | flops | bytes accessed | tf_op | source)
XLA Modules:
  0.0 173.1 jit_solution(4469907977472782720)
XLA Ops:
  0.0 168.5 %exchange.1 = (f32[1024,4096]{1,0:T(8,128)S(1)}, bf16[8,4,32,1024]{3,2,1,0:T(8,128)(2,1)S(1)}, bf16[1024,256]{1,0:T(8,128)(2,1)S(1)}) custom-call(s32[16]{0:T(128)} %idx_hbm.1, f32[2,2,2,4]{3,2,1,0:T(2,128)} %bitcast.2, f32[2,2,2,4]{3,2,1,0:T(2,128)} %bitcast.3, bf16[16,2,8192]{2,1,0:T(2,128)(2,1)} %left_hbm.1, bf16[16,2,4096]{2,1,0:T(2,128)(2,1)} %right_hbm.1, ...), custom_call_target="tpu_custom_call" | custom-call | tf_op jit(solution)/shard_map/exchange/pallas_call | solution.py:367
  168.5 4.6 %finish.1 = bf16[2,512,4096]{2,1,0:T(8,128)(2,1)} custom-call(f32[1024,4096]{1,0:T(8,128)S(1)} %get-tuple-element.8.total_ref, bf16[8,4,32,1024]{3,2,1,0:T(8,128)(2,1)S(1)} %get-tuple-element.9.last_ref, bf16[1024,256]{1,0:T(8,128)(2,1)S(1)} %get-tuple-element.10.lhs_ref), custom_call_target="tpu_custom_call" | custom-call | tf_op jit(solution)/shard_map/finish/pallas_call | solution.py:409

commit v4 on v3

--- a/solution.py
+++ b/solution.py
@@ -10,6 +10,7 @@
 MESH = pl.DeviceIdType.MESH
 F32 = jnp.float32
 BF16 = jnp.bfloat16
+PIECES = 4
 VMEM_LIMIT = 24 * 1024 * 1024
 NT = (((1,), (1,)), ((), ()))
 TN = (((0,), (0,)), ((), ()))
@@ -187,27 +188,39 @@
 
     gather_steps = (half - 1, half)
     group = chips // 4
-    slice_cols = wide // pieces
-
-    def add_slice(g, piece, j):
-        at = pl.ds(pl.multiple_of(j * slice_cols, slice_cols), slice_cols)
+    quarter = half // 4
+    slice_cols = wide // quarter
+    lead = pieces // 2
+
+    def add_slice(g, phase, j):
+        n = phase * pieces + j
+        piece = n // quarter
+        first = lax.rem(n, quarter) * slice_cols
+        at = pl.ds(pl.multiple_of(first, slice_cols), slice_cols)
         right = early[g * group : (g + 1) * group, piece, :, at].reshape(-1, slice_cols)
-        to = pl.ds(pl.multiple_of(piece * wide + j * slice_cols, slice_cols), slice_cols)
+        to = pl.ds(pl.multiple_of(n * slice_cols, slice_cols), slice_cols)
         more = dot(lhs_now[...], right)
         total_ref[:, to] = more if g == 0 else total_ref[:, to] + more
 
-    def gather_step(s, work=None):
-        @pl.loop(0, pieces)
+    def gather_piece(d, s, j):
+        if 1 <= s <= gather_steps[d]:
+            gather_copy(d, s - 1, j).wait_recv()
+        if s < gather_steps[d]:
+            gather_copy(d, s, j).start()
+
+    def gather_half(s, second, work=None):
+        @pl.loop(0, lead)
         def _(j):
-            for d in range(2):
-                if 1 <= s <= gather_steps[d]:
-                    gather_copy(d, s - 1, j).wait_recv()
-                if s < gather_steps[d]:
-                    gather_copy(d, s, j).start()
+            gather_piece(0, s, j + lead if second else j)
+            gather_piece(1, s + 1 if second else s, j if second else j + lead)
             if work is not None:
-                add_slice(*work, j)
-
-    gather_step(0)
+                add_slice(*work, j + lead if second else j)
+
+    @pl.loop(0, pieces)
+    def _(j):
+        for d in range(2):
+            gather_piece(d, 0, j)
+
     for load in loads[4:]:
         load.wait()
 
@@ -268,17 +281,28 @@
         handed.append((n, there))
         own_blocks[n] = src[...]
 
-    def block_step(s):
-        for d in range(2):
-            if 1 <= s <= len(counts[d]):
-                block_copy(d, s - 1).wait_recv()
-            if s < len(counts[d]):
-                block_copy(d, s).start()
-            if s == 0 and d == 0:
-                hand_over(lsend.at[0], 0)
-            if 1 <= s <= len(counts[d]):
-                at = bases[d][s - 1] + (0 if d == 0 else counts[d][s - 1] - 1)
-                hand_over(landing[d].at[at], slot_of(d, s) if s < half else chips - 1)
+    def block_step(d, s):
+        if 1 <= s <= len(counts[d]):
+            block_copy(d, s - 1).wait_recv()
+        if s < len(counts[d]):
+            block_copy(d, s).start()
+        if 1 <= s <= len(counts[d]):
+            at = bases[d][s - 1] + (0 if d == 0 else counts[d][s - 1] - 1)
+            hand_over(landing[d].at[at], slot_of(d, s) if s < half else chips - 1)
+
+    due = {}
+    for d in range(2):
+        for s in range(1, len(counts[d]) + 1):
+            late = s - (half - 3)
+            if d == 0:
+                when = (s, 1) if late < 0 else ((half - 3, 0), (half - 2, 0), (half - 1, 0), (half - 1, 1))[late]
+            else:
+                when = (s, 0) if late < 0 else ((half - 4, 1), (half - 3, 1), (half - 2, 1))[late]
+            due.setdefault(when, []).append((d, s))
+
+    def pass_blocks(s, part):
+        for which in due.get((s, part), ()):
+            block_step(*which)
 
     krow, kcol = grid2(16 * 2 * group, 16 * 2 * group)
     imag = (krow // 8) % 2 == 1
@@ -297,18 +321,33 @@
         to_ref[0 : block.shape[1]] = dot(block, signed, TN).astype(BF16)
         to_ref[block.shape[1] :] = dot(block, crossed, TN).astype(BF16)
 
-    block_step(0)
-    quarter = half // 4
-    for s in range(1, half + 1):
+    block_step(0, 0)
+    hand_over(lsend.at[0], 0)
+    block_step(1, 0)
+
+    @pl.loop(0, lead)
+    def _(j):
+        gather_piece(1, 1, j)
+
+    pass_blocks(0, 1)
+    for s in range(1, half):
         ready, phase = divmod(s - 1, quarter)
-        if s == half:
-            block_step(s)
-            build_lhs(3, lhs_ref)
         if phase == 0 and ready >= 1:
             build_lhs(ready - 1, lhs_now)
-        gather_step(s, (ready - 1, phase) if ready >= 1 else None)
-        if s < half:
-            block_step(s)
+        work = (ready - 1, phase) if ready >= 1 else None
+        for part in range(2):
+            gather_half(s, part, work)
+            pass_blocks(s, part)
+    ready, phase = divmod(half - 1, quarter)
+    if phase == 0:
+        build_lhs(ready - 1, lhs_now)
+
+    @pl.loop(0, pieces)
+    def _(j):
+        add_slice(ready - 1, phase, j)
+
+    build_lhs(3, lhs_ref)
+    gather_half(half, 0)
 
     give_right.wait_send()
     give_left.wait_send()
@@ -354,7 +393,7 @@
     mine = paths // 2
     lrows, rrows = left_slabs.shape[2] // 128, right_slabs.shape[2] // 128
     half = chips // 2
-    pieces = half // 4
+    pieces = PIECES
     cols = rrows * 128
     block = 2 * lrows * 128 // chips
     vmem = pl.BlockSpec(memory_space=pltpu.VMEM)

time: 175 us -> 172 us (0.983)
  Pallas kernels: 173 us -> 171 us
    pallas_call x1, Pallas kernels: 168 us -> 167 us  [shards(): pl.pallas_call(functools.partial(exchange_kernel, chips), out_shape=(jax....]
where the time goes in v4:
time: 172 us; the launch traced here: 171 us
  Pallas kernels  171 us (99%)
    pallas_call x1, Pallas kernels, shards(): pl.pallas_call(functools.partial(exchange_kernel, chips), out_shape=(jax....  167 us
    pallas_call x1, Pallas kernels, shards(): pl.pallas_call(finish_kernel, out_shape=jax.ShapeDtypeStruct((2, block, c...  4.6 us

profile of v4, /device:TPU:38, one launch (start us, length us, event | category | flops | bytes accessed | tf_op | source)
XLA Modules:
  0.0 171.3 jit_solution(1431173225403802549)
XLA Ops:
  0.0 166.7 %exchange.1 = (f32[1024,4096]{1,0:T(8,128)S(1)}, bf16[8,4,32,1024]{3,2,1,0:T(8,128)(2,1)S(1)}, bf16[1024,256]{1,0:T(8,128)(2,1)S(1)}) custom-call(s32[16]{0:T(128)} %idx_hbm.1, f32[2,2,2,4]{3,2,1,0:T(2,128)} %bitcast.2, f32[2,2,2,4]{3,2,1,0:T(2,128)} %bitcast.3, bf16[16,2,8192]{2,1,0:T(2,128)(2,1)} %left_hbm.1, bf16[16,2,4096]{2,1,0:T(2,128)(2,1)} %right_hbm.1, ...), custom_call_target="tpu_custom_call" | custom-call | tf_op jit(solution)/shard_map/exchange/pallas_call | solution.py:406
  166.7 4.6 %finish.1 = bf16[2,512,4096]{2,1,0:T(8,128)(2,1)} custom-call(f32[1024,4096]{1,0:T(8,128)S(1)} %get-tuple-element.8.total_ref, bf16[8,4,32,1024]{3,2,1,0:T(8,128)(2,1)S(1)} %get-tuple-element.9.last_ref, bf16[1024,256]{1,0:T(8,128)(2,1)S(1)} %get-tuple-element.10.lhs_ref), custom_call_target="tpu_custom_call" | custom-call | tf_op jit(solution)/shard_map/finish/pallas_call | solution.py:448
